TPU v7x, 32 devices: a whole 2x2x4 slice. The times are simulated.
32 devices in a mesh: seq: 16 (over z, x, core), res: 2 (over y).
Axes of the slice: x: 2, y: 2, z: 4, core: 2. Of those that a mesh axis runs over, the one named last changes fastest.
Arguments:
- alignment_rows: bfloat16 [1024, 16, 64], P('seq', 'res'), may hold values from -6 to 6
- pair_features: bfloat16 [16, 16, 128], P('res', 'seq'), may hold values from -6 to 6
- sequence_block_count: int32 [16], P('seq'), may hold values from 16 to 64
- cluster_member_count: int32 [1024], P('seq'), may hold values from 1 to 16
- residue_present_mask: int32 [16], replicated, may hold values 0 or 1
- attention_in_weight: bfloat16 [64, 256], replicated, may hold values from -0.75 to 0.75
- attention_out_weight: bfloat16 [64, 64], replicated, may hold values from -4 to 4
- pair_bias_weight: float32 [128, 8], replicated, may hold values from -48 to 48
- outer_factor_weight: bfloat16 [64, 64], replicated, may hold values from -0.75 to 0.75
- outer_output_weight: float32 [1024, 128], replicated, may hold values from -4 to 4
- outer_product_bias: float32 [128], replicated, may hold values from -3 to 3
Outputs:
- row_attention_update: bfloat16 [1024, 16, 64], P('seq', 'res')
- pair_update: bfloat16 [16, 16, 128], P('seq', 'res')
All inputs are finite; a program needn't handle non-finite values.
Results may differ from a plain program's by a relative error of at most 0.0081.
Values may be sent and summed in bfloat16 or wider, within the bound.
A program may use at most 64 MiB of HBM per device.

v0:
```python
import functools
import math

import jax
import jax.numpy as jnp
from jax import lax
from jax.experimental import pallas as pl
from jax.experimental.pallas import tpu as pltpu
from jax.sharding import PartitionSpec as P

MESH = pl.DeviceIdType.MESH
F32 = jnp.float32
BF16 = jnp.bfloat16
LANES = 128


def dot(a, b, ca, cb, precision=None):
    return lax.dot_general(
        a, b, (((ca,), (cb,)), ((), ())), precision=precision, preferred_element_type=F32
    )


def norm_over(values, axis):
    centre = jnp.mean(values, axis=axis, keepdims=True)
    shifted = values - centre
    spread = jnp.mean(shifted * shifted, axis=axis, keepdims=True)
    return shifted * lax.rsqrt(spread + 1e-05)


def kernel(
    n_seq,
    n_res,
    slots,
    rl,
    heads,
    factor,
    count_ref,
    mask_ref,
    x_ref,
    pair_ref,
    members_ref,
    w_in_ref,
    w_out_ref,
    w_bias_ref,
    w_fac_ref,
    w_proj_hbm,
    bias_ref,
    update_ref,
    pair_out_ref,
    rows32,
    x_t,
    xn_buf,
    xn_recv,
    tile_buf,
    tile_recv,
    q_s,
    kv_s,
    roll_s,
    gate_s,
    bias_s,
    ctx_s,
    left_buf,
    left_recv,
    right_s,
    outer_s,
    w_raw,
    w_perm,
    part_buf,
    part_recv,
    w_sem,
    xn_send_sem,
    xn_recv_sem,
    tile_send_sem,
    tile_recv_sem,
    left_send_sem,
    left_recv_sem,
    part_send_sem,
    part_recv_sem,
):
    me_s = lax.axis_index("seq")
    me_r = lax.axis_index("res")
    width = x_ref.shape[2]
    hd = width // heads
    tiles = rl // 2
    n_keys = rl * n_res
    row_block = n_keys // n_seq
    key_block = pair_ref.shape[0] // rl

    def seq_peer(k):
        return lax.rem(me_s + k, n_seq)

    def res_peer(k):
        return lax.rem(me_r + k, n_res)

    barrier = pltpu.get_barrier_semaphore()

    @pl.loop(1, n_seq)
    def _(k):
        pl.semaphore_signal(barrier, inc=1, device_id=(seq_peer(k), me_r), device_id_type=MESH)

    for k in range(1, n_res):
        pl.semaphore_signal(barrier, inc=1, device_id=(me_s, res_peer(k)), device_id_type=MESH)

    w_copy = pltpu.make_async_copy(w_proj_hbm, w_raw, w_sem)
    w_copy.start()

    lane = lax.broadcasted_iota(jnp.int32, (1, LANES), 1)
    low = lane < slots
    count = count_ref[0]
    usable = (lax.rem(lane, slots) < count).astype(F32)
    members = members_ref[...].astype(F32)
    members = jnp.concatenate([members, members], axis=1)
    seq_weight = members * usable
    own_weight = jnp.sum(jnp.where(low, seq_weight, 0.0), axis=1, keepdims=True)

    pair_norm = norm_over(pair_ref[...].astype(F32), 1)
    pad = jnp.zeros((LANES - pair_norm.shape[0], pair_norm.shape[1]), F32)
    bias_t = dot(
        w_bias_ref[...], jnp.concatenate([pair_norm, pad], axis=0), 1, 1, lax.Precision.HIGHEST
    )
    tile_buf[...] = jnp.where(lane == LANES - 1, own_weight, bias_t)

    rows32[:, :width] = x_ref[...].astype(F32).reshape(slots * rl, width)
    eye = (
        lax.broadcasted_iota(jnp.int32, (width, width), 0)
        == lax.broadcasted_iota(jnp.int32, (width, width), 1)
    ).astype(F32).astype(BF16)
    for t in range(tiles):
        pair_rows = jnp.concatenate(
            [rows32[pl.ds(2 * t + e, slots, stride=rl), :][:, :width] for e in range(2)], axis=0
        ).astype(BF16)
        turned = dot(eye, pair_rows, 1, 1)
        x_t[t] = turned
        xn_buf[t] = norm_over(turned, 0).astype(BF16)

    pl.semaphore_wait(barrier, n_seq - 1 + n_res - 1)

    xn_copies = [
        pltpu.make_async_remote_copy(
            src_ref=xn_buf,
            dst_ref=xn_recv.at[k - 1],
            send_sem=xn_send_sem.at[k - 1],
            recv_sem=xn_recv_sem.at[k - 1],
            device_id=(me_s, res_peer(k)),
            device_id_type=MESH,
        )
        for k in range(1, n_res)
    ]
    for copy in xn_copies:
        copy.start()

    def tile_copy(k):
        return pltpu.make_async_remote_copy(
            src_ref=tile_buf,
            dst_ref=tile_recv.at[me_s],
            send_sem=tile_send_sem.at[k - 1],
            recv_sem=tile_recv_sem.at[k - 1],
            device_id=(seq_peer(k), me_r),
            device_id_type=MESH,
        )

    @pl.loop(1, n_seq)
    def _(k):
        tile_copy(k).start()

    tile_recv[me_s] = tile_buf[...]

    scale = 1.0 / math.sqrt(hd)

    def put_kv(block, t, kv):
        kv = kv.astype(BF16).astype(F32)
        kv_s[block, t] = kv
        roll_s[block, t] = pltpu.roll(kv, slots, 1)

    for t in range(tiles):
        proj = dot(w_in_ref[...], xn_buf[t], 0, 0)
        q_s[t] = (proj[:width] * scale).astype(BF16).astype(F32)
        put_kv(0, t, proj[width : 3 * width])
        gate_s[t] = jax.nn.sigmoid(proj[3 * width :])

    w_copy.wait()
    for d in range(factor):
        w_perm[d * factor : (d + 1) * factor] = w_raw[pl.ds(d, factor, stride=factor), :].astype(BF16)

    @pl.loop(1, n_seq)
    def _(k):
        tile_copy(k).wait()

    weight_sum = jnp.sum(tile_recv[...], axis=0)[:, LANES - 1 : LANES]

    def res_of(block):
        return lax.rem(me_r + n_res - block, n_res)

    for block in range(n_res):
        for u in range(tiles):
            keyed = []
            for e in range(2):
                j = res_of(block) * rl + 2 * u + e
                key_mask = jnp.where(mask_ref[j] == 1, 0.0, -1000000.0).astype(F32)
                tile = tile_recv[j // key_block] + key_mask
                j_in = j % key_block if key_block > 1 else 0
                if key_block > 1:
                    picks = [
                        jnp.sum(
                            jnp.where(lane == i * key_block + j_in, tile, 0.0), axis=1, keepdims=True
                        )
                        for i in range(rl)
                    ]
                else:
                    picks = [tile[:, i : i + 1] for i in range(rl)]
                keyed.append([jnp.broadcast_to(p, (heads, LANES)) for p in picks])
            for t in range(tiles):
                bias_s[t, 0, block, u] = jnp.where(low, keyed[0][2 * t], keyed[1][2 * t + 1])
                bias_s[t, 1, block, u] = jnp.where(low, keyed[1][2 * t], keyed[0][2 * t + 1])

    for block in range(1, n_res):
        xn_copies[block - 1].wait()
        for t in range(tiles):
            put_kv(block, t, dot(w_in_ref[:, width : 3 * width], xn_recv[block - 1, t], 0, 0))

    def heads_of(ref, base, d):
        return ref[pl.ds(base + d, heads, stride=hd), :]

    for t in range(tiles):
        queries = [q_s.at[t][pl.ds(d, heads, stride=hd), :] for d in range(hd)]
        scores = []
        for turn in range(2):
            source = roll_s if turn else kv_s
            for block in range(n_res):
                for u in range(tiles):
                    total = queries[0] * heads_of(source.at[block, u], 0, 0)
                    for d in range(1, hd):
                        total = total + queries[d] * heads_of(source.at[block, u], 0, d)
                    scores.append(total + bias_s[t, turn, block, u])
        top = functools.reduce(jnp.maximum, scores)
        expo = [jnp.exp(s - top) for s in scores]
        norm = 1.0 / functools.reduce(jnp.add, expo)
        probs = [(e * norm).astype(BF16).astype(F32) for e in expo]
        context = [None] * hd
        at = 0
        for turn in range(2):
            source = roll_s if turn else kv_s
            for block in range(n_res):
                for u in range(tiles):
                    for d in range(hd):
                        term = probs[at] * heads_of(source.at[block, u], width, d)
                        context[d] = term if context[d] is None else context[d] + term
                    at += 1
        for d in range(hd):
            ctx_s[t, pl.ds(d, heads, stride=hd), :] = context[d]

    gated_tiles = []
    keep_tiles = []
    for t in range(tiles):
        gated = (gate_s[t] * ctx_s[t]).astype(BF16)
        gated_tiles.append(gated)
        update = dot(w_out_ref[...], gated, 0, 0).astype(BF16).astype(F32) * usable
        outer_norm = norm_over(x_t[t] + update, 0).astype(BF16)
        factors = dot(w_fac_ref[...], outer_norm, 0, 0)
        keeps = [(mask_ref[me_r * rl + 2 * t + e]).astype(F32) for e in range(2)]
        keep = jnp.where(low, keeps[0], keeps[1])
        left_buf[t] = (factors[:factor] * keep).astype(BF16)
        right = factors[factor:] * keep * seq_weight
        turned = pltpu.roll(right, slots, 1)
        zero = jnp.zeros_like(right)
        right_s[0, pl.ds(2 * t, factor, stride=rl), :] = jnp.where(low, right, zero)
        right_s[0, pl.ds(2 * t + 1, factor, stride=rl), :] = jnp.where(low, turned, zero)
        right_s[1, pl.ds(2 * t, factor, stride=rl), :] = jnp.where(low, zero, turned)
        right_s[1, pl.ds(2 * t + 1, factor, stride=rl), :] = jnp.where(low, zero, right)

    left_copies = [
        pltpu.make_async_remote_copy(
            src_ref=left_buf,
            dst_ref=left_recv.at[k - 1],
            send_sem=left_send_sem.at[k - 1],
            recv_sem=left_recv_sem.at[k - 1],
            device_id=(me_s, res_peer(k)),
            device_id_type=MESH,
        )
        for k in range(1, n_res)
    ]
    for copy in left_copies:
        copy.start()

    right_all = right_s[...].reshape(2 * factor * rl, LANES).astype(BF16)
    groups = LANES // factor
    even = lax.rem(lane // factor, 2) == 0

    def project(block, left):
        products = dot(right_all, left.reshape(tiles * factor, LANES), 1, 1)
        for half in range(2):
            for g in range(factor // groups):
                base = (half * factor + g * groups) * rl
                a = [products[base + k * rl : base + (k + 1) * rl] for k in range(groups)]
                p0 = jnp.where(low, a[0], pltpu.roll(a[2], 64, 1))
                p2 = jnp.where(low, pltpu.roll(a[0], 64, 1), a[2])
                p1 = jnp.where(low, a[1], pltpu.roll(a[3], 64, 1))
                p3 = jnp.where(low, pltpu.roll(a[1], 64, 1), a[3])
                out = [
                    jnp.where(even, p0, pltpu.roll(p1, 32, 1)),
                    jnp.where(even, pltpu.roll(p0, 96, 1), p1),
                    jnp.where(even, p2, pltpu.roll(p3, 32, 1)),
                    jnp.where(even, pltpu.roll(p2, 96, 1), p3),
                ]
                for ip in range(groups):
                    i = 2 * ip + half
                    outer_s[i * rl : (i + 1) * rl, g * LANES : (g + 1) * LANES] = out[ip]
        part = dot(outer_s[...].astype(BF16), w_perm[...], 1, 0)
        part_buf[pl.ds(res_of(block) * rl, rl)] = part.reshape(rl, rl, part.shape[1])

    project(0, left_buf[...])

    row = lax.broadcasted_iota(jnp.int32, (slots, 1), 0)
    row_usable = (row < count).astype(F32)
    w_out_wide = jnp.concatenate([w_out_ref[...], w_out_ref[...]], axis=1)
    for t in range(tiles):
        plain = dot(gated_tiles[t], w_out_wide, 0, 0).astype(BF16).astype(F32)
        for e in range(2):
            rows32[pl.ds(2 * t + e, slots, stride=rl), :] = (
                plain[e * slots : (e + 1) * slots] * row_usable
            )
    update_ref[...] = rows32[:, :width].reshape(slots, rl, width).astype(BF16)

    for block in range(1, n_res):
        left_copies[block - 1].wait()
        project(block, left_recv[block - 1])

    def part_copy(k):
        owner = seq_peer(k)
        return pltpu.make_async_remote_copy(
            src_ref=part_buf.at[pl.ds(owner * row_block, row_block)],
            dst_ref=part_recv.at[k - 1],
            send_sem=part_send_sem.at[k - 1],
            recv_sem=part_recv_sem.at[k - 1],
            device_id=(owner, me_r),
            device_id_type=MESH,
        )

    @pl.loop(1, n_seq)
    def _(k):
        part_copy(k).start()

    @pl.loop(1, n_seq)
    def _(k):
        part_copy(k).wait()

    total = part_buf[pl.ds(me_s * row_block, row_block)] + jnp.sum(part_recv[...], axis=0)
    pair_out_ref[...] = (total / weight_sum[None] + bias_ref[...][None]).astype(BF16)


def solution(mesh):
    n_seq = mesh.shape["seq"]
    n_res = mesh.shape["res"]

    def local(
        alignment_rows,
        pair_features,
        sequence_block_count,
        cluster_member_count,
        residue_present_mask,
        attention_in_weight,
        attention_out_weight,
        pair_bias_weight,
        outer_factor_weight,
        outer_output_weight,
        outer_product_bias,
    ):
        slots, rl, width = alignment_rows.shape
        heads = pair_bias_weight.shape[1]
        factor = outer_factor_weight.shape[1] // 2
        pair_width = outer_output_weight.shape[1]
        key_block = pair_features.shape[1]
        row_block = rl * n_res // n_seq
        tiles = rl // 2
        assert 2 * slots == LANES and tiles * factor == LANES and 4 * factor == LANES
        assert pair_width == LANES and heads == 8 and rl == 8
        vmem = pl.BlockSpec(memory_space=pltpu.VMEM)
        smem = pl.BlockSpec(memory_space=pltpu.SMEM)
        dma = pltpu.SemaphoreType.DMA
        return pl.pallas_call(
            functools.partial(kernel, n_seq, n_res, slots, rl, heads, factor),
            out_shape=(
                jax.ShapeDtypeStruct((slots, rl, width), BF16),
                jax.ShapeDtypeStruct((row_block, rl, pair_width), BF16),
            ),
            in_specs=[smem, smem] + [vmem] * 7 + [pl.BlockSpec(memory_space=pl.ANY), vmem],
            out_specs=(vmem, vmem),
            scratch_shapes=[
                pltpu.VMEM((slots * rl, LANES), F32),
                pltpu.VMEM((tiles, width, LANES), F32),
                pltpu.VMEM((tiles, width, LANES), BF16),
                pltpu.VMEM((n_res - 1, tiles, width, LANES), BF16),
                pltpu.VMEM((heads, LANES), F32),
                pltpu.VMEM((n_seq, heads, LANES), F32),
                pltpu.VMEM((tiles, width, LANES), F32),
                pltpu.VMEM((n_res, tiles, 2 * width, LANES), F32),
                pltpu.VMEM((n_res, tiles, 2 * width, LANES), F32),
                pltpu.VMEM((tiles, width, LANES), F32),
                pltpu.VMEM((tiles, 2, n_res, tiles, heads, LANES), F32),
                pltpu.VMEM((tiles, width, LANES), F32),
                pltpu.VMEM((tiles, factor, LANES), BF16),
                pltpu.VMEM((n_res - 1, tiles, factor, LANES), BF16),
                pltpu.VMEM((2, factor * rl, LANES), F32),
                pltpu.VMEM((rl * rl, factor * factor), F32),
                pltpu.VMEM((factor * factor, pair_width), F32),
                pltpu.VMEM((factor * factor, pair_width), BF16),
                pltpu.VMEM((rl * n_res, rl, pair_width), F32),
                pltpu.VMEM((n_seq - 1, row_block, rl, pair_width), F32),
                dma,
                dma((n_res - 1,)),
                dma((n_res - 1,)),
                dma((n_seq - 1,)),
                dma((n_seq - 1,)),
                dma((n_res - 1,)),
                dma((n_res - 1,)),
                dma((n_seq - 1,)),
                dma((n_seq - 1,)),
            ],
            compiler_params=pltpu.CompilerParams(collective_id=0, has_side_effects=True),
        )(
            sequence_block_count,
            residue_present_mask,
            alignment_rows,
            pair_features.reshape(rl * key_block, pair_features.shape[2]),
            cluster_member_count.reshape(1, slots),
            attention_in_weight,
            attention_out_weight,
            pair_bias_weight.T,
            outer_factor_weight,
            outer_output_weight,
            outer_product_bias.reshape(1, pair_width),
        )

    return jax.shard_map(
        local,
        mesh=mesh,
        in_specs=(
            P("seq", "res", None),
            P("res", "seq", None),
            P("seq"),
            P("seq"),
            P(),
            P(),
            P(),
            P(),
            P(),
            P(),
            P(),
        ),
        out_specs=(P("seq", "res", None), P("seq", "res", None)),
        check_vma=False,
    )
```

profile of v0, /device:TPU:0, one launch (start us, length us, event | category | flops | bytes accessed | tf_op | source)
XLA Modules:
  0.0 25.8 jit_solution(10083033341592962310)
XLA Ops:
  1.3 22.4 %shard_map.122 = (bf16[64,8,64]{2,1,0:T(8,128)(2,1)}, bf16[1,8,128]{2,1,0:T(8,128)(2,1)}) custom-call(s32[1]{0:T(128)S(6)} %copy.15.count_ref, s32[16]{0:T(128)} %mask_ref.1, bf16[64,8,64]{2,1,0:T(8,128)(2,1)} %x_ref.1, bf16[8,128]{1,0:T(8,128)(2,1)} %bitcast.5, s32[1,64]{1,0:T(1,128)} %bitcast.6, bf16[64,256]{1,0:T(8,128)(2,1)} %w_in_ref.1, ...), custom_call_target="tpu_custom_call" | custom-call | tf_op jit(solution)/shard_map/pallas_call | solution.py:380
  23.7 0.0 copy-start
  23.7 1.6 %copy.16 = bf16[64,8,64]{2,1,0:T(8,128)(2,1)} copy(bf16[64,8,64]{2,1,0:T(8,128)(2,1)} %get-tuple-element.4) | data formatting | bytes 131072
  25.2 0.0 copy-done
  25.2 0.6 %copy.17 = bf16[1,8,128]{2,1,0:T(8,128)(2,1)} copy(bf16[1,8,128]{2,1,0:T(8,128)(2,1)S(1)} %copy-done) | data formatting | bytes 4096
Async XLA Ops:
  23.7 1.6 %copy-start = (bf16[1,8,128]{2,1,0:T(8,128)(2,1)S(1)}, bf16[1,8,128]{2,1,0:T(8,128)(2,1)}, u32[]{:S(2)}) copy-start(bf16[1,8,128]{2,1,0:T(8,128)(2,1)} %get-tuple-element.5) | copy-start | bytes 6148
where the time goes:
time: 26 us; the launch traced here: 25.8 us
  Pallas kernels  22.4 us (86%)
  local copies, waits for them, and re-layouts  2.15 us (8%)
  between operations  1.3 us (5%)
    pallas_call x1, Pallas kernels, local(): pl.pallas_call(functools.partial(kernel, n_seq, n_res, slots, rl, heads,...  22.4 us
    unnamed x4, local copies, waits for them, and re-layouts  2.15 us

commit v1 on v0

v1 whole, which is shorter than its diff:
```python
import functools
import math

import jax
import jax.numpy as jnp
from jax import lax
from jax.experimental import pallas as pl
from jax.experimental.pallas import tpu as pltpu
from jax.sharding import PartitionSpec as P

MESH = pl.DeviceIdType.MESH
F32 = jnp.float32
BF16 = jnp.bfloat16
LANES = 128


def dot(a, b, ca, cb, precision=None):
    return lax.dot_general(
        a, b, (((ca,), (cb,)), ((), ())), precision=precision, preferred_element_type=F32
    )


def norm_over(values, axis):
    centre = jnp.mean(values, axis=axis, keepdims=True)
    shifted = values - centre
    spread = jnp.mean(shifted * shifted, axis=axis, keepdims=True)
    return shifted * lax.rsqrt(spread + 1e-05)


def iota(shape, axis):
    return lax.broadcasted_iota(jnp.int32, shape, axis)


def ones_where(mask):
    return jnp.where(mask, 1.0, 0.0).astype(BF16)


def each(start, stop, body):
    if stop - start <= 16:
        for k in range(start, stop):
            body(k)
    else:
        pl.loop(start, stop)(body)


def kernel(
    n_seq,
    n_res,
    slots,
    rl,
    heads,
    factor,
    count_hbm,
    mask_hbm,
    x_hbm,
    pair_hbm,
    members_hbm,
    w_in_hbm,
    w_out_hbm,
    w_bias_hbm,
    w_fac_hbm,
    w_proj_hbm,
    bias_hbm,
    update_ref,
    pair_out_ref,
    count_ref,
    mask_ref,
    x_ref,
    pair_ref,
    members_ref,
    w_in_ref,
    w_out_ref,
    w_bias_ref,
    w_fac_ref,
    w_raw,
    bias_ref,
    rows32,
    x_t,
    xn_buf,
    xn_recv,
    tile_buf,
    tile_recv,
    pick_s,
    w_in_t,
    w_out_t,
    w_out_p,
    w_fac_t,
    kv_s,
    roll_s,
    gate_s,
    score_s,
    gated_s,
    left_buf,
    left_recv,
    right_s,
    outer_s,
    w_perm,
    part_buf,
    part_recv,
    in_sem,
    xn_send_sem,
    xn_recv_sem,
    tile_send_sem,
    tile_recv_sem,
    left_send_sem,
    left_recv_sem,
    part_send_sem,
    part_recv_sem,
):
    me_s = lax.axis_index("seq")
    me_r = lax.axis_index("res")
    width = x_ref.shape[2]
    hd = width // heads
    tiles = rl // 2
    row_block = rl * n_res // n_seq

    def seq_peer(k):
        return lax.rem(me_s + k, n_seq)

    def res_peer(k):
        return lax.rem(me_r + k, n_res)

    def res_of(block):
        return lax.rem(me_r + n_res - block, n_res)

    barrier = pltpu.get_barrier_semaphore()

    def greet(k):
        pl.semaphore_signal(barrier, inc=1, device_id=(seq_peer(k), me_r), device_id_type=MESH)

    each(1, n_seq, greet)
    for k in range(1, n_res):
        pl.semaphore_signal(barrier, inc=1, device_id=(me_s, res_peer(k)), device_id_type=MESH)

    loads = {}
    for at, (name, src, dst) in enumerate(
        [
            ("pair", pair_hbm, pair_ref),
            ("w_bias", w_bias_hbm, w_bias_ref),
            ("count", count_hbm, count_ref),
            ("members", members_hbm, members_ref),
            ("x", x_hbm, x_ref),
            ("w_in", w_in_hbm, w_in_ref),
            ("mask", mask_hbm, mask_ref),
            ("w_out", w_out_hbm, w_out_ref),
            ("w_fac", w_fac_hbm, w_fac_ref),
            ("w_proj", w_proj_hbm, w_raw),
            ("bias", bias_hbm, bias_ref),
        ]
    ):
        loads[name] = pltpu.make_async_copy(src, dst, in_sem.at[at])
        loads[name].start()

    def loaded(*names):
        for name in names:
            loads[name].wait()

    lane = iota((1, LANES), 1)
    low = lane < slots
    of_head = iota((heads, LANES), 1) // rl == iota((heads, LANES), 0)

    loaded("pair", "w_bias", "count", "members")
    count = count_ref[0]
    usable = (lax.rem(lane, slots) < count).astype(F32)
    members = members_ref[...].astype(F32)
    members = jnp.concatenate([members, members], axis=1)
    seq_weight = members * usable
    own_weight = jnp.sum(jnp.where(low, seq_weight, 0.0), axis=1, keepdims=True)

    pair_norm = norm_over(pair_ref[...].astype(F32), 1)
    bias_t = dot(
        w_bias_ref[...],
        jnp.concatenate([pair_norm] * (LANES // rl), axis=0),
        1,
        1,
        lax.Precision.HIGHEST,
    )
    packed = jnp.sum(jnp.where(of_head, bias_t, 0.0), axis=0, keepdims=True)
    packed = jnp.where(lane == LANES - 1, own_weight, packed)
    tile_buf[...] = packed
    tile_recv[me_s] = packed

    loaded("x")
    rows32[:, :width] = x_ref[...].astype(F32).reshape(slots * rl, width)
    eye = ones_where(iota((width, width), 0) == iota((width, width), 1))
    for t in range(tiles):
        pair_rows = jnp.concatenate(
            [rows32[pl.ds(2 * t + e, slots, stride=rl), :][:, :width] for e in range(2)], axis=0
        ).astype(BF16)
        turned = dot(eye, pair_rows, 1, 1)
        x_t[t] = turned
        xn_buf[t] = norm_over(turned, 0).astype(BF16)

    pl.semaphore_wait(barrier, n_seq - 1 + n_res - 1)

    def tile_copy(k):
        return pltpu.make_async_remote_copy(
            src_ref=tile_buf,
            dst_ref=tile_recv.at[me_s],
            send_sem=tile_send_sem.at[k - 1],
            recv_sem=tile_recv_sem.at[k - 1],
            device_id=(seq_peer(k), me_r),
            device_id_type=MESH,
        )

    each(1, n_seq, lambda k: tile_copy(k).start())

    xn_copies = [
        pltpu.make_async_remote_copy(
            src_ref=xn_buf,
            dst_ref=xn_recv.at[k - 1],
            send_sem=xn_send_sem.at[k - 1],
            recv_sem=xn_recv_sem.at[k - 1],
            device_id=(me_s, res_peer(k)),
            device_id_type=MESH,
        )
        for k in range(1, n_res)
    ]
    for copy in xn_copies:
        copy.start()

    loaded("w_in", "mask", "w_out", "w_fac", "w_proj", "bias")
    groups_in = w_in_ref.shape[1]
    to_row, from_col = iota((groups_in, groups_in), 0), iota((groups_in, groups_in), 1)
    order = (
        to_row // width * width
        + lax.rem(to_row, heads) * hd
        + lax.rem(to_row, width) // heads
    )
    perm = ones_where(order == from_col)
    w_in_t[...] = dot(perm, w_in_ref[...], 1, 1).astype(BF16)
    perm_out = perm[:width, :width]
    w_out_t[...] = dot(w_out_ref[...], perm_out, 0, 1).astype(BF16)
    w_out_p[...] = dot(perm_out, w_out_ref[...], 1, 0).astype(BF16)
    w_fac_t[...] = dot(w_fac_ref[...], eye, 0, 0).astype(BF16)

    row_k, col_l = iota((2 * LANES, LANES), 0), iota((2 * LANES, LANES), 1)
    half = (col_l >= slots).astype(jnp.int32)
    for t in range(tiles):
        for turn in range(2):
            hit = (lax.rem(row_k, rl) == 2 * t + half) & (
                row_k // LANES == (half if turn == 0 else 1 - half)
            )
            pick_s[t, :, turn * LANES : (turn + 1) * LANES] = ones_where(hit)

    scale = 1.0 / math.sqrt(hd)

    def put_kv(block, t, kv):
        kv = kv.astype(BF16).astype(F32)
        kv_s[block, t] = kv
        roll_s[block, t] = pltpu.roll(kv, slots, 1)

    queries = []
    for t in range(tiles):
        proj = dot(w_in_t[...], xn_buf[t], 1, 0)
        queries.append((proj[:width] * scale).astype(BF16).astype(F32))
        put_kv(0, t, proj[width : 3 * width])
        gate_s[t] = jax.nn.sigmoid(proj[3 * width :])

    for d in range(factor):
        w_perm[d * factor : (d + 1) * factor] = w_raw[pl.ds(d, factor, stride=factor), :].astype(BF16)

    combos = [(turn, block, u) for turn in range(2) for block in range(n_res) for u in range(tiles)]

    def score(block):
        for at, (turn, of, u) in enumerate(combos):
            if of != block:
                continue
            source = (roll_s if turn else kv_s).at[block, u]
            for t in range(tiles):
                total = None
                for d in range(hd):
                    term = queries[t][d * heads : (d + 1) * heads] * source[d * heads : (d + 1) * heads]
                    total = term if total is None else total + term
                score_s[t, at] = total

    score(0)
    for block in range(1, n_res):
        xn_copies[block - 1].wait()
        for t in range(tiles):
            put_kv(block, t, dot(w_in_t[width : 3 * width], xn_recv[block - 1, t], 1, 0))
        score(block)

    each(1, n_seq, lambda k: tile_copy(k).wait())

    weight_sum = jnp.sum(tile_recv[...], axis=0)[:, LANES - 1 : LANES]
    keyed = []
    for block in range(n_res):
        for u in range(tiles):
            sides = []
            for e in range(2):
                j = res_of(block) * rl + 2 * u + e
                key_mask = jnp.where(mask_ref[j] == 1, 0.0, -1000000.0).astype(F32)
                sides.append(jnp.where(of_head, tile_recv[j] + key_mask, 0.0))
            keyed.append(jnp.concatenate(sides, axis=1))
    keyed = jnp.concatenate(keyed, axis=0)
    pieces = []
    rest = keyed
    for _ in range(3):
        piece = rest.astype(BF16)
        pieces.append(piece)
        rest = rest - piece.astype(F32)
    pieces = jnp.concatenate(pieces, axis=0)
    n_rows = keyed.shape[0]

    left_copies = []
    for k in range(1, n_res):
        left_copies.append(
            [
                pltpu.make_async_remote_copy(
                    src_ref=left_buf.at[t],
                    dst_ref=left_recv.at[k - 1, t],
                    send_sem=left_send_sem.at[k - 1, t],
                    recv_sem=left_recv_sem.at[k - 1, t],
                    device_id=(me_s, res_peer(k)),
                    device_id_type=MESH,
                )
                for t in range(tiles)
            ]
        )

    rights = []
    for t in range(tiles):
        spread = dot(pieces, pick_s[t], 1, 0)
        spread = (spread[:n_rows] + spread[n_rows : 2 * n_rows]) + spread[2 * n_rows :]
        scores = []
        for at, (turn, block, u) in enumerate(combos):
            row = (block * tiles + u) * heads
            scores.append(
                score_s[t, at] + spread[row : row + heads, turn * LANES : (turn + 1) * LANES]
            )
        top = functools.reduce(jnp.maximum, scores)
        context = [None] * hd
        mass = None
        for at, (turn, block, u) in enumerate(combos):
            source = (roll_s if turn else kv_s).at[block, u]
            expo = jnp.exp(scores[at] - top)
            mass = expo if mass is None else mass + expo
            for d in range(hd):
                term = expo * source[width + d * heads : width + (d + 1) * heads]
                context[d] = term if context[d] is None else context[d] + term
        norm = 1.0 / mass
        context = jnp.concatenate([c * norm for c in context], axis=0)
        gated = (gate_s[t] * context).astype(BF16)
        gated_s[t] = gated
        update = dot(w_out_t[...], gated, 1, 0).astype(BF16).astype(F32) * usable
        outer_norm = norm_over(x_t[t] + update, 0).astype(BF16)
        factors = dot(w_fac_t[...], outer_norm, 1, 0)
        keeps = [(mask_ref[me_r * rl + 2 * t + e]).astype(F32) for e in range(2)]
        keep = jnp.where(low, keeps[0], keeps[1])
        left_buf[t] = (factors[:factor] * keep).astype(BF16)
        for copies in left_copies:
            copies[t].start()
        rights.append(factors[factor:] * keep * seq_weight)

    for t in range(tiles):
        right = rights[t]
        turned = pltpu.roll(right, slots, 1)
        zero = jnp.zeros_like(right)
        right_s[0, pl.ds(2 * t, factor, stride=rl), :] = jnp.where(low, right, zero)
        right_s[0, pl.ds(2 * t + 1, factor, stride=rl), :] = jnp.where(low, turned, zero)
        right_s[1, pl.ds(2 * t, factor, stride=rl), :] = jnp.where(low, zero, turned)
        right_s[1, pl.ds(2 * t + 1, factor, stride=rl), :] = jnp.where(low, zero, right)

    right_all = right_s[...].reshape(2 * factor * rl, LANES).astype(BF16)
    groups = LANES // factor
    even = lax.rem(lane // factor, 2) == 0

    def project(block, left):
        products = dot(right_all, left.reshape(tiles * factor, LANES), 1, 1)
        for half in range(2):
            for g in range(factor // groups):
                base = (half * factor + g * groups) * rl
                a = [products[base + k * rl : base + (k + 1) * rl] for k in range(groups)]
                p0 = jnp.where(low, a[0], pltpu.roll(a[2], 64, 1))
                p2 = jnp.where(low, pltpu.roll(a[0], 64, 1), a[2])
                p1 = jnp.where(low, a[1], pltpu.roll(a[3], 64, 1))
                p3 = jnp.where(low, pltpu.roll(a[1], 64, 1), a[3])
                out = [
                    jnp.where(even, p0, pltpu.roll(p1, 32, 1)),
                    jnp.where(even, pltpu.roll(p0, 96, 1), p1),
                    jnp.where(even, p2, pltpu.roll(p3, 32, 1)),
                    jnp.where(even, pltpu.roll(p2, 96, 1), p3),
                ]
                for ip in range(groups):
                    i = 2 * ip + half
                    outer_s[i * rl : (i + 1) * rl, g * LANES : (g + 1) * LANES] = out[ip]
        part = dot(outer_s[...].astype(BF16), w_perm[...], 1, 0)
        part_buf[pl.ds(res_of(block) * rl, rl)] = part.reshape(rl, rl, part.shape[1]).astype(BF16)

    def part_copy(owner, k):
        return pltpu.make_async_remote_copy(
            src_ref=part_buf.at[pl.ds(owner * row_block, row_block)],
            dst_ref=part_recv.at[k - 1],
            send_sem=part_send_sem.at[k - 1],
            recv_sem=part_recv_sem.at[k - 1],
            device_id=(owner, me_r),
            device_id_type=MESH,
        )

    def send_parts(block):
        for m in range(rl // row_block):
            owner = res_of(block) * (rl // row_block) + m
            offset = lax.rem(owner + n_seq - me_s, n_seq)

            @pl.when(offset > 0)
            def _():
                part_copy(owner, offset).start()

    project(0, left_buf[...])
    send_parts(0)
    for block in range(1, n_res):
        for t in range(tiles):
            left_copies[block - 1][t].wait()
        project(block, left_recv[block - 1])
        send_parts(block)

    row_usable = (iota((slots, 1), 0) < count).astype(F32)
    w_out_wide = jnp.concatenate([w_out_p[...], w_out_p[...]], axis=1)
    for t in range(tiles):
        plain = dot(gated_s[t], w_out_wide, 0, 0).astype(BF16).astype(F32)
        for e in range(2):
            rows32[pl.ds(2 * t + e, slots, stride=rl), :] = (
                plain[e * slots : (e + 1) * slots] * row_usable
            )
    update_ref[...] = rows32[:, :width].reshape(slots, rl, width).astype(BF16)

    each(1, n_seq, lambda k: part_copy(seq_peer(k), k).wait())

    own = part_buf[pl.ds(me_s * row_block, row_block)].astype(F32)
    total = own + jnp.sum(part_recv[...].astype(F32), axis=0)
    pair_out_ref[...] = (total / weight_sum[None] + bias_ref[...][None]).astype(BF16)


def finish(update_ref, pair_ref, update_hbm, pair_hbm, sem):
    copies = [
        pltpu.make_async_copy(update_ref, update_hbm, sem.at[0]),
        pltpu.make_async_copy(pair_ref, pair_hbm, sem.at[1]),
    ]
    for copy in copies:
        copy.start()
    for copy in copies:
        copy.wait()


def solution(mesh):
    n_seq = mesh.shape["seq"]
    n_res = mesh.shape["res"]

    def local(
        alignment_rows,
        pair_features,
        sequence_block_count,
        cluster_member_count,
        residue_present_mask,
        attention_in_weight,
        attention_out_weight,
        pair_bias_weight,
        outer_factor_weight,
        outer_output_weight,
        outer_product_bias,
    ):
        slots, rl, width = alignment_rows.shape
        heads = pair_bias_weight.shape[1]
        factor = outer_factor_weight.shape[1] // 2
        pair_width = outer_output_weight.shape[1]
        key_block = pair_features.shape[1]
        row_block = rl * n_res // n_seq
        tiles = rl // 2
        n_combos = 2 * n_res * tiles
        assert 2 * slots == LANES and tiles * factor == LANES and 4 * factor == LANES
        assert pair_width == LANES and heads == 8 and rl == 8
        assert key_block == 1 and rl % row_block == 0 and heads * rl < LANES
        any_space = pl.BlockSpec(memory_space=pltpu.HBM)
        vmem = pl.BlockSpec(memory_space=pltpu.VMEM)
        dma = pltpu.SemaphoreType.DMA
        operands = (
            sequence_block_count,
            residue_present_mask,
            alignment_rows,
            pair_features.reshape(rl, pair_features.shape[2]),
            cluster_member_count.reshape(1, slots),
            attention_in_weight,
            attention_out_weight,
            pair_bias_weight.T,
            outer_factor_weight,
            outer_output_weight,
            outer_product_bias.reshape(1, pair_width),
        )
        update, pair_update = pl.pallas_call(
            functools.partial(kernel, n_seq, n_res, slots, rl, heads, factor),
            out_shape=(
                pltpu.VMEM((slots, rl, width), BF16),
                pltpu.VMEM((row_block, rl, pair_width), BF16),
            ),
            in_specs=[any_space] * len(operands),
            out_specs=(vmem, vmem),
            scratch_shapes=[
                (pltpu.SMEM if at < 2 else pltpu.VMEM)(value.shape, value.dtype)
                for at, value in enumerate(operands)
            ]
            + [
                pltpu.VMEM((slots * rl, LANES), F32),
                pltpu.VMEM((tiles, width, LANES), F32),
                pltpu.VMEM((tiles, width, LANES), BF16),
                pltpu.VMEM((n_res - 1, tiles, width, LANES), BF16),
                pltpu.VMEM((1, LANES), F32),
                pltpu.VMEM((n_seq, 1, LANES), F32),
                pltpu.VMEM((tiles, 2 * LANES, 2 * LANES), BF16),
                pltpu.VMEM((4 * width, width), BF16),
                pltpu.VMEM((width, width), BF16),
                pltpu.VMEM((width, width), BF16),
                pltpu.VMEM((width, width), BF16),
                pltpu.VMEM((n_res, tiles, 2 * width, LANES), F32),
                pltpu.VMEM((n_res, tiles, 2 * width, LANES), F32),
                pltpu.VMEM((tiles, width, LANES), F32),
                pltpu.VMEM((tiles, n_combos, heads, LANES), F32),
                pltpu.VMEM((tiles, width, LANES), BF16),
                pltpu.VMEM((tiles, factor, LANES), BF16),
                pltpu.VMEM((n_res - 1, tiles, factor, LANES), BF16),
                pltpu.VMEM((2, factor * rl, LANES), F32),
                pltpu.VMEM((rl * rl, factor * factor), F32),
                pltpu.VMEM((factor * factor, pair_width), BF16),
                pltpu.VMEM((rl * n_res, rl, pair_width), BF16),
                pltpu.VMEM((n_seq - 1, row_block, rl, pair_width), BF16),
                dma((len(operands),)),
                dma((n_res - 1,)),
                dma((n_res - 1,)),
                dma((n_seq - 1,)),
                dma((n_seq - 1,)),
                dma((n_res - 1, tiles)),
                dma((n_res - 1, tiles)),
                dma((n_seq - 1,)),
                dma((n_seq - 1,)),
            ],
            compiler_params=pltpu.CompilerParams(collective_id=0, has_side_effects=True),
        )(*operands)
        return pl.pallas_call(
            finish,
            out_shape=(
                jax.ShapeDtypeStruct(update.shape, BF16),
                jax.ShapeDtypeStruct(pair_update.shape, BF16),
            ),
            in_specs=[vmem, vmem],
            out_specs=(any_space, any_space),
            scratch_shapes=[dma((2,))],
        )(
            pltpu.with_memory_space_constraint(update, pltpu.VMEM),
            pltpu.with_memory_space_constraint(pair_update, pltpu.VMEM),
        )

    return jax.shard_map(
        local,
        mesh=mesh,
        in_specs=(
            P("seq", "res", None),
            P("res", "seq", None),
            P("seq"),
            P("seq"),
            P(),
            P(),
            P(),
            P(),
            P(),
            P(),
            P(),
        ),
        out_specs=(P("seq", "res", None), P("seq", "res", None)),
        check_vma=False,
    )
```

time: 26 us -> 20.6 us (0.79)
  the two profiles are of different devices: /device:TPU:0 before, /device:TPU:5 now
where the time goes in v1:
time: 20.6 us; the launch traced here: 20.5 us
  Pallas kernels  19.2 us (93%)
  between operations  1.29 us (6%)
    pallas_call x1, Pallas kernels, local(): pl.pallas_call(functools.partial(kernel, n_seq, n_res, slots, rl, heads,...  18.5 us
    pallas_call x1, Pallas kernels, local(): pl.pallas_call(finish, out_shape=(jax.ShapeDtypeStruct(update.shape, BF16...  0.68 us

profile of v1, /device:TPU:5, one launch (start us, length us, event | category | flops | bytes accessed | tf_op | source)
XLA Modules:
  0.0 20.5 jit_solution(17084073425097360446)
XLA Ops:
  1.3 18.5 %shard_map.122 = (bf16[64,8,64]{2,1,0:T(8,128)(2,1)S(1)}, bf16[1,8,128]{2,1,0:T(8,128)(2,1)S(1)}) custom-call(s32[1]{0:T(128)S(6)} %copy.13.count_hbm, s32[16]{0:T(128)} %mask_hbm.1, bf16[64,8,64]{2,1,0:T(8,128)(2,1)} %x_hbm.1, bf16[8,128]{1,0:T(8,128)(2,1)} %bitcast.5, s32[1,64]{1,0:T(1,128)} %bitcast.6, bf16[64,256]{1,0:T(8,128)(2,1)} %w_in_hbm.1, ...), custom_call_target="tpu_custom_call" | custom-call | tf_op jit(solution)/shard_map/pallas_call | solution.py:490
  19.8 0.7 %shard_map.123 = (bf16[64,8,64]{2,1,0:T(8,128)(2,1)}, bf16[1,8,128]{2,1,0:T(8,128)(2,1)}) custom-call(bf16[64,8,64]{2,1,0:T(8,128)(2,1)S(1)} %get-tuple-element.4.update_ref, bf16[1,8,128]{2,1,0:T(8,128)(2,1)S(1)} %get-tuple-element.5.pair_ref), custom_call_target="tpu_custom_call" | custom-call | tf_op jit(solution)/shard_map/pallas_call | solution.py:538

commit v2 on v1

--- a/solution.py
+++ b/solution.py
@@ -41,6 +41,10 @@
             body(k)
     else:
         pl.loop(start, stop)(body)
+
+
+def drain(ref, sem):
+    pltpu.make_async_copy(ref, ref, sem).wait()
 
 
 def kernel(
@@ -80,7 +84,6 @@
     xn_recv,
     tile_buf,
     tile_recv,
-    pick_s,
     w_in_t,
     w_out_t,
     w_out_p,
@@ -93,7 +96,6 @@
     left_buf,
     left_recv,
     right_s,
-    outer_s,
     w_perm,
     part_buf,
     part_recv,
@@ -178,46 +180,47 @@
     packed = jnp.sum(jnp.where(of_head, bias_t, 0.0), axis=0, keepdims=True)
     packed = jnp.where(lane == LANES - 1, own_weight, packed)
     tile_buf[...] = packed
-    tile_recv[me_s] = packed
+    tile_recv[0] = packed
 
     loaded("x")
     rows32[:, :width] = x_ref[...].astype(F32).reshape(slots * rl, width)
     eye = ones_where(iota((width, width), 0) == iota((width, width), 1))
+    all_rows = jnp.concatenate(
+        [rows32[pl.ds(i, slots, stride=rl), :][:, :width] for i in range(rl)], axis=0
+    ).astype(BF16)
+    turned = dot(eye, all_rows, 1, 1)
+    x_t[...] = turned
+    x_norm = norm_over(turned, 0).astype(BF16)
     for t in range(tiles):
-        pair_rows = jnp.concatenate(
-            [rows32[pl.ds(2 * t + e, slots, stride=rl), :][:, :width] for e in range(2)], axis=0
-        ).astype(BF16)
-        turned = dot(eye, pair_rows, 1, 1)
-        x_t[t] = turned
-        xn_buf[t] = norm_over(turned, 0).astype(BF16)
+        xn_buf[t] = x_norm[:, t * LANES : (t + 1) * LANES]
 
     pl.semaphore_wait(barrier, n_seq - 1 + n_res - 1)
 
-    def tile_copy(k):
-        return pltpu.make_async_remote_copy(
+    def tile_send(k):
+        pltpu.make_async_remote_copy(
             src_ref=tile_buf,
-            dst_ref=tile_recv.at[me_s],
-            send_sem=tile_send_sem.at[k - 1],
-            recv_sem=tile_recv_sem.at[k - 1],
+            dst_ref=tile_recv.at[k],
+            send_sem=tile_send_sem,
+            recv_sem=tile_recv_sem,
             device_id=(seq_peer(k), me_r),
             device_id_type=MESH,
-        )
-
-    each(1, n_seq, lambda k: tile_copy(k).start())
-
-    xn_copies = [
-        pltpu.make_async_remote_copy(
-            src_ref=xn_buf,
-            dst_ref=xn_recv.at[k - 1],
-            send_sem=xn_send_sem.at[k - 1],
-            recv_sem=xn_recv_sem.at[k - 1],
+        ).start()
+
+    each(1, n_seq, tile_send)
+
+    def xn_copy(k, t):
+        return pltpu.make_async_remote_copy(
+            src_ref=xn_buf.at[t],
+            dst_ref=xn_recv.at[k - 1, t],
+            send_sem=xn_send_sem,
+            recv_sem=xn_recv_sem.at[k - 1, t],
             device_id=(me_s, res_peer(k)),
             device_id_type=MESH,
         )
-        for k in range(1, n_res)
-    ]
-    for copy in xn_copies:
-        copy.start()
+
+    for k in range(1, n_res):
+        for t in range(tiles):
+            xn_copy(k, t).start()
 
     loaded("w_in", "mask", "w_out", "w_fac", "w_proj", "bias")
     groups_in = w_in_ref.shape[1]
@@ -234,15 +237,6 @@
     w_out_p[...] = dot(perm_out, w_out_ref[...], 1, 0).astype(BF16)
     w_fac_t[...] = dot(w_fac_ref[...], eye, 0, 0).astype(BF16)
 
-    row_k, col_l = iota((2 * LANES, LANES), 0), iota((2 * LANES, LANES), 1)
-    half = (col_l >= slots).astype(jnp.int32)
-    for t in range(tiles):
-        for turn in range(2):
-            hit = (lax.rem(row_k, rl) == 2 * t + half) & (
-                row_k // LANES == (half if turn == 0 else 1 - half)
-            )
-            pick_s[t, :, turn * LANES : (turn + 1) * LANES] = ones_where(hit)
-
     scale = 1.0 / math.sqrt(hd)
 
     def put_kv(block, t, kv):
@@ -250,21 +244,21 @@
         kv_s[block, t] = kv
         roll_s[block, t] = pltpu.roll(kv, slots, 1)
 
-    queries = []
+    proj = dot(w_in_t[...], jnp.concatenate([xn_buf[t] for t in range(tiles)], axis=1), 1, 0)
+    query = (proj[:width] * scale).astype(BF16).astype(F32)
+    gate_s[...] = jax.nn.sigmoid(proj[3 * width :])
+    queries = [query[:, t * LANES : (t + 1) * LANES] for t in range(tiles)]
     for t in range(tiles):
-        proj = dot(w_in_t[...], xn_buf[t], 1, 0)
-        queries.append((proj[:width] * scale).astype(BF16).astype(F32))
-        put_kv(0, t, proj[width : 3 * width])
-        gate_s[t] = jax.nn.sigmoid(proj[3 * width :])
+        put_kv(0, t, proj[width : 3 * width, t * LANES : (t + 1) * LANES])
 
     for d in range(factor):
         w_perm[d * factor : (d + 1) * factor] = w_raw[pl.ds(d, factor, stride=factor), :].astype(BF16)
 
     combos = [(turn, block, u) for turn in range(2) for block in range(n_res) for u in range(tiles)]
 
-    def score(block):
+    def score(block, key_tile):
         for at, (turn, of, u) in enumerate(combos):
-            if of != block:
+            if of != block or u != key_tile:
                 continue
             source = (roll_s if turn else kv_s).at[block, u]
             for t in range(tiles):
@@ -274,61 +268,38 @@
                     total = term if total is None else total + term
                 score_s[t, at] = total
 
-    score(0)
+    for u in range(tiles):
+        score(0, u)
     for block in range(1, n_res):
-        xn_copies[block - 1].wait()
-        for t in range(tiles):
-            put_kv(block, t, dot(w_in_t[width : 3 * width], xn_recv[block - 1, t], 1, 0))
-        score(block)
-
-    each(1, n_seq, lambda k: tile_copy(k).wait())
+        for u in range(tiles):
+            xn_copy(block, u).wait_recv()
+            put_kv(block, u, dot(w_in_t[width : 3 * width], xn_recv[block - 1, u], 1, 0))
+            score(block, u)
+
+    drain(tile_recv.at[pl.ds(1, n_seq - 1)], tile_recv_sem)
 
     weight_sum = jnp.sum(tile_recv[...], axis=0)[:, LANES - 1 : LANES]
-    keyed = []
+    head_base = iota((heads, LANES), 0) * rl
+    side = (iota((heads, LANES), 1) >= slots).astype(jnp.int32)
+    picks = [head_base + 2 * t + side for t in range(tiles)]
+
+    keyed = {}
     for block in range(n_res):
-        for u in range(tiles):
-            sides = []
-            for e in range(2):
-                j = res_of(block) * rl + 2 * u + e
-                key_mask = jnp.where(mask_ref[j] == 1, 0.0, -1000000.0).astype(F32)
-                sides.append(jnp.where(of_head, tile_recv[j] + key_mask, 0.0))
-            keyed.append(jnp.concatenate(sides, axis=1))
-    keyed = jnp.concatenate(keyed, axis=0)
-    pieces = []
-    rest = keyed
-    for _ in range(3):
-        piece = rest.astype(BF16)
-        pieces.append(piece)
-        rest = rest - piece.astype(F32)
-    pieces = jnp.concatenate(pieces, axis=0)
-    n_rows = keyed.shape[0]
-
-    left_copies = []
-    for k in range(1, n_res):
-        left_copies.append(
-            [
-                pltpu.make_async_remote_copy(
-                    src_ref=left_buf.at[t],
-                    dst_ref=left_recv.at[k - 1, t],
-                    send_sem=left_send_sem.at[k - 1, t],
-                    recv_sem=left_recv_sem.at[k - 1, t],
-                    device_id=(me_s, res_peer(k)),
-                    device_id_type=MESH,
-                )
-                for t in range(tiles)
-            ]
-        )
-
-    rights = []
+        for i in range(rl):
+            j = res_of(block) * rl + i
+            key_mask = jnp.where(mask_ref[j] == 1, 0.0, -1000000.0).astype(F32)
+            row = tile_recv[lax.rem(me_s - j + n_seq, n_seq)] + key_mask
+            keyed[block, i] = jnp.broadcast_to(row, (heads, LANES))
+
     for t in range(tiles):
-        spread = dot(pieces, pick_s[t], 1, 0)
-        spread = (spread[:n_rows] + spread[n_rows : 2 * n_rows]) + spread[2 * n_rows :]
+        spread = {
+            key: jnp.take_along_axis(row, picks[t], axis=1, mode="promise_in_bounds")
+            for key, row in keyed.items()
+        }
         scores = []
         for at, (turn, block, u) in enumerate(combos):
-            row = (block * tiles + u) * heads
-            scores.append(
-                score_s[t, at] + spread[row : row + heads, turn * LANES : (turn + 1) * LANES]
-            )
+            near, far = spread[block, 2 * u + turn], spread[block, 2 * u + 1 - turn]
+            scores.append(score_s[t, at] + jnp.where(low, near, far))
         top = functools.reduce(jnp.maximum, scores)
         context = [None] * hd
         mass = None
@@ -341,59 +312,89 @@
                 context[d] = term if context[d] is None else context[d] + term
         norm = 1.0 / mass
         context = jnp.concatenate([c * norm for c in context], axis=0)
-        gated = (gate_s[t] * context).astype(BF16)
-        gated_s[t] = gated
-        update = dot(w_out_t[...], gated, 1, 0).astype(BF16).astype(F32) * usable
-        outer_norm = norm_over(x_t[t] + update, 0).astype(BF16)
-        factors = dot(w_fac_t[...], outer_norm, 1, 0)
-        keeps = [(mask_ref[me_r * rl + 2 * t + e]).astype(F32) for e in range(2)]
-        keep = jnp.where(low, keeps[0], keeps[1])
-        left_buf[t] = (factors[:factor] * keep).astype(BF16)
-        for copies in left_copies:
-            copies[t].start()
-        rights.append(factors[factor:] * keep * seq_weight)
-
+        gated_s[t] = (gate_s[:, t * LANES : (t + 1) * LANES] * context).astype(BF16)
+
+    all_usable = jnp.concatenate([usable] * tiles, axis=1)
+    keeps = [mask_ref[me_r * rl + i].astype(F32) for i in range(rl)]
+    all_keep = jnp.concatenate(
+        [jnp.where(low, keeps[2 * t], keeps[2 * t + 1]) for t in range(tiles)], axis=1
+    )
+    gated = jnp.concatenate([gated_s[t] for t in range(tiles)], axis=1)
+    update = dot(w_out_t[...], gated, 1, 0).astype(BF16).astype(F32) * all_usable
+    outer_norm = norm_over(x_t[...] + update, 0).astype(BF16)
+    factors = dot(w_fac_t[...], outer_norm, 1, 0) * all_keep
+    left = factors[:factor].astype(BF16)
     for t in range(tiles):
-        right = rights[t]
+        left_buf[t] = left[:, t * LANES : (t + 1) * LANES]
+
+    def left_copy(k):
+        return pltpu.make_async_remote_copy(
+            src_ref=left_buf,
+            dst_ref=left_recv.at[k - 1],
+            send_sem=left_send_sem,
+            recv_sem=left_recv_sem.at[k - 1],
+            device_id=(me_s, res_peer(k)),
+            device_id_type=MESH,
+        )
+
+    for k in range(1, n_res):
+        left_copy(k).start()
+
+    for t in range(tiles):
+        right = factors[factor:, t * LANES : (t + 1) * LANES] * seq_weight
         turned = pltpu.roll(right, slots, 1)
-        zero = jnp.zeros_like(right)
-        right_s[0, pl.ds(2 * t, factor, stride=rl), :] = jnp.where(low, right, zero)
-        right_s[0, pl.ds(2 * t + 1, factor, stride=rl), :] = jnp.where(low, turned, zero)
-        right_s[1, pl.ds(2 * t, factor, stride=rl), :] = jnp.where(low, zero, turned)
-        right_s[1, pl.ds(2 * t + 1, factor, stride=rl), :] = jnp.where(low, zero, right)
-
-    right_all = right_s[...].reshape(2 * factor * rl, LANES).astype(BF16)
+        right_s[0, pl.ds(2 * t, factor, stride=rl), :] = right
+        right_s[0, pl.ds(2 * t + 1, factor, stride=rl), :] = turned
+        right_s[1, pl.ds(2 * t, factor, stride=rl), :] = turned
+        right_s[1, pl.ds(2 * t + 1, factor, stride=rl), :] = right
+
     groups = LANES // factor
-    even = lax.rem(lane // factor, 2) == 0
+    sides = []
+    for pair in range(groups // 2):
+        rows = []
+        for g in range(factor // groups):
+            at = (g * groups + 2 * pair) * rl
+            rows.append(jnp.where(low, right_s[0, at : at + rl], right_s[1, at + rl : at + 2 * rl]))
+        sides.append(jnp.concatenate(rows, axis=0))
+    right_all = jnp.concatenate(sides, axis=1).astype(BF16)
 
     def project(block, left):
-        products = dot(right_all, left.reshape(tiles * factor, LANES), 1, 1)
-        for half in range(2):
-            for g in range(factor // groups):
-                base = (half * factor + g * groups) * rl
-                a = [products[base + k * rl : base + (k + 1) * rl] for k in range(groups)]
-                p0 = jnp.where(low, a[0], pltpu.roll(a[2], 64, 1))
-                p2 = jnp.where(low, pltpu.roll(a[0], 64, 1), a[2])
-                p1 = jnp.where(low, a[1], pltpu.roll(a[3], 64, 1))
-                p3 = jnp.where(low, pltpu.roll(a[1], 64, 1), a[3])
-                out = [
-                    jnp.where(even, p0, pltpu.roll(p1, 32, 1)),
-                    jnp.where(even, pltpu.roll(p0, 96, 1), p1),
-                    jnp.where(even, p2, pltpu.roll(p3, 32, 1)),
-                    jnp.where(even, pltpu.roll(p2, 96, 1), p3),
-                ]
-                for ip in range(groups):
-                    i = 2 * ip + half
-                    outer_s[i * rl : (i + 1) * rl, g * LANES : (g + 1) * LANES] = out[ip]
-        part = dot(outer_s[...].astype(BF16), w_perm[...], 1, 0)
+        blank = jnp.zeros((factor, LANES), BF16)
+        outer = []
+        for t in range(tiles):
+            plain = left[t].astype(F32)
+            turned = pltpu.roll(plain, slots, 1)
+            spread = []
+            for first, second in ((plain, turned), (turned, plain)):
+                near = jnp.where(low, first, 0.0).astype(BF16)
+                far = jnp.where(low, 0.0, second).astype(BF16)
+                for pair in range(groups // 2):
+                    for piece in (near, far):
+                        cells = [blank] * (groups // 2)
+                        cells[pair] = piece
+                        spread.append(jnp.concatenate(cells, axis=1))
+            spread = jnp.concatenate(spread, axis=0)
+            products = dot(right_all, spread, 1, 1)
+            for e in range(2):
+                outer.append(
+                    jnp.concatenate(
+                        [
+                            products[g * rl : (g + 1) * rl, e * LANES : (e + 1) * LANES]
+                            for g in range(factor // groups)
+                        ],
+                        axis=1,
+                    )
+                )
+        outer = jnp.concatenate(outer, axis=0).astype(BF16)
+        part = dot(outer, w_perm[...], 1, 0)
         part_buf[pl.ds(res_of(block) * rl, rl)] = part.reshape(rl, rl, part.shape[1]).astype(BF16)
 
     def part_copy(owner, k):
         return pltpu.make_async_remote_copy(
             src_ref=part_buf.at[pl.ds(owner * row_block, row_block)],
             dst_ref=part_recv.at[k - 1],
-            send_sem=part_send_sem.at[k - 1],
-            recv_sem=part_recv_sem.at[k - 1],
+            send_sem=part_send_sem,
+            recv_sem=part_recv_sem,
             device_id=(owner, me_r),
             device_id_type=MESH,
         )
@@ -410,8 +411,7 @@
     project(0, left_buf[...])
     send_parts(0)
     for block in range(1, n_res):
-        for t in range(tiles):
-            left_copies[block - 1][t].wait()
+        left_copy(block).wait_recv()
         project(block, left_recv[block - 1])
         send_parts(block)
 
@@ -425,7 +425,11 @@
             )
     update_ref[...] = rows32[:, :width].reshape(slots, rl, width).astype(BF16)
 
-    each(1, n_seq, lambda k: part_copy(seq_peer(k), k).wait())
+    drain(tile_recv.at[pl.ds(1, n_seq - 1)], tile_send_sem)
+    drain(xn_recv, xn_send_sem)
+    drain(left_recv, left_send_sem)
+    drain(part_recv, part_recv_sem)
+    drain(part_recv, part_send_sem)
 
     own = part_buf[pl.ds(me_s * row_block, row_block)].astype(F32)
     total = own + jnp.sum(part_recv[...].astype(F32), axis=0)
@@ -501,37 +505,35 @@
             ]
             + [
                 pltpu.VMEM((slots * rl, LANES), F32),
-                pltpu.VMEM((tiles, width, LANES), F32),
+                pltpu.VMEM((width, tiles * LANES), F32),
                 pltpu.VMEM((tiles, width, LANES), BF16),
                 pltpu.VMEM((n_res - 1, tiles, width, LANES), BF16),
                 pltpu.VMEM((1, LANES), F32),
                 pltpu.VMEM((n_seq, 1, LANES), F32),
-                pltpu.VMEM((tiles, 2 * LANES, 2 * LANES), BF16),
                 pltpu.VMEM((4 * width, width), BF16),
                 pltpu.VMEM((width, width), BF16),
                 pltpu.VMEM((width, width), BF16),
                 pltpu.VMEM((width, width), BF16),
                 pltpu.VMEM((n_res, tiles, 2 * width, LANES), F32),
                 pltpu.VMEM((n_res, tiles, 2 * width, LANES), F32),
-                pltpu.VMEM((tiles, width, LANES), F32),
+                pltpu.VMEM((width, tiles * LANES), F32),
                 pltpu.VMEM((tiles, n_combos, heads, LANES), F32),
                 pltpu.VMEM((tiles, width, LANES), BF16),
                 pltpu.VMEM((tiles, factor, LANES), BF16),
                 pltpu.VMEM((n_res - 1, tiles, factor, LANES), BF16),
                 pltpu.VMEM((2, factor * rl, LANES), F32),
-                pltpu.VMEM((rl * rl, factor * factor), F32),
                 pltpu.VMEM((factor * factor, pair_width), BF16),
                 pltpu.VMEM((rl * n_res, rl, pair_width), BF16),
                 pltpu.VMEM((n_seq - 1, row_block, rl, pair_width), BF16),
                 dma((len(operands),)),
+                dma,
+                dma((n_res - 1, tiles)),
+                dma,
+                dma,
+                dma,
                 dma((n_res - 1,)),
-                dma((n_res - 1,)),
-                dma((n_seq - 1,)),
-                dma((n_seq - 1,)),
-                dma((n_res - 1, tiles)),
-                dma((n_res - 1, tiles)),
-                dma((n_seq - 1,)),
-                dma((n_seq - 1,)),
+                dma,
+                dma,
             ],
             compiler_params=pltpu.CompilerParams(collective_id=0, has_side_effects=True),
         )(*operands)

time: 20.6 us -> 18.8 us (0.913)
  Pallas kernels: 19.2 us -> 17.3 us
    pallas_call x1, Pallas kernels: 18.5 us -> 16.7 us  [local(): pl.pallas_call(functools.partial(kernel, n_seq, n_res, slots, rl, heads,...]
where the time goes in v2:
time: 18.8 us; the launch traced here: 18.6 us
  Pallas kernels  17.3 us (92%)
  between operations  1.29 us (7%)
    pallas_call x1, Pallas kernels, local(): pl.pallas_call(functools.partial(kernel, n_seq, n_res, slots, rl, heads,...  16.7 us
    pallas_call x1, Pallas kernels, local(): pl.pallas_call(finish, out_shape=(jax.ShapeDtypeStruct(update.shape, BF16...  0.68 us

profile of v2, /device:TPU:5, one launch (start us, length us, event | category | flops | bytes accessed | tf_op | source)
XLA Modules:
  0.0 18.6 jit_solution(15390950601755675999)
XLA Ops:
  1.3 16.7 %shard_map.122 = (bf16[64,8,64]{2,1,0:T(8,128)(2,1)S(1)}, bf16[1,8,128]{2,1,0:T(8,128)(2,1)S(1)}) custom-call(s32[1]{0:T(128)S(6)} %copy.13.count_hbm, s32[16]{0:T(128)} %mask_hbm.1, bf16[64,8,64]{2,1,0:T(8,128)(2,1)} %x_hbm.1, bf16[8,128]{1,0:T(8,128)(2,1)} %bitcast.5, s32[1,64]{1,0:T(1,128)} %bitcast.6, bf16[64,256]{1,0:T(8,128)(2,1)} %w_in_hbm.1, ...), custom_call_target="tpu_custom_call" | custom-call | tf_op jit(solution)/shard_map/pallas_call | solution.py:494
  18.0 0.7 %shard_map.123 = (bf16[64,8,64]{2,1,0:T(8,128)(2,1)}, bf16[1,8,128]{2,1,0:T(8,128)(2,1)}) custom-call(bf16[64,8,64]{2,1,0:T(8,128)(2,1)S(1)} %get-tuple-element.4.update_ref, bf16[1,8,128]{2,1,0:T(8,128)(2,1)S(1)} %get-tuple-element.5.pair_ref), custom_call_target="tpu_custom_call" | custom-call | tf_op jit(solution)/shard_map/pallas_call | solution.py:540
